TPU v7x, 32 devices: a whole 2x2x4 slice. The times are simulated.
32 devices in a mesh: dp: 4 (over x, core), context: 2 (over y), tensor: 4 (over z).
Axes of the slice: x: 2, y: 2, z: 4, core: 2. Of those that a mesh axis runs over, the one named last changes fastest.
Arguments:
- tokens: bfloat16 [12, 512, 1536], P('dp', 'context')
- cotangent: bfloat16 [12, 512, 1536], P('dp', 'context'), may hold values from -6 to 6
- segments: int32 [12, 512], P('dp'), may hold values from 0 to 3, as said below
- positions: int32 [12, 512], P('dp', 'context'), may hold values from 0 to 255, as said below
- norm_attn: bfloat16 [1536], replicated, may hold values from 0.099609375 to 1.8984375
- w_query: bfloat16 [1536, 1536], P(None, 'tensor')
- key_weight: bfloat16 [1536, 768], P(None, 'tensor')
- value_weight: bfloat16 [1536, 768], P(None, 'tensor'), may hold values from -0.15625 to 0.15625
- w_out: bfloat16 [1536, 1536], P('tensor'), may hold values from -0.875 to 0.875
- norm_ffn: bfloat16 [1536], replicated, may hold values from 0.099609375 to 1.8984375
- w_gate: bfloat16 [1536, 4096], P(None, 'tensor'), may hold values from -0.15625 to 0.15625
- w_up: bfloat16 [1536, 4096], P(None, 'tensor'), may hold values from -0.15625 to 0.15625
- w_down: bfloat16 [4096, 1536], P('tensor'), may hold values from -0.09375 to 0.09375
Outputs:
- block_out: bfloat16 [12, 512, 1536], P('dp', 'context')
- input_grad: bfloat16 [12, 512, 1536], P('dp', 'context')
- attn_gain_grad: float32 [1536], replicated
- query_grad: float32 [1536, 1536], P(None, 'tensor')
- key_grad: float32 [1536, 768], P(None, 'tensor')
- value_grad: float32 [1536, 768], P(None, 'tensor')
- out_grad: float32 [1536, 1536], P('tensor')
- ffn_gain_grad: float32 [1536], replicated
- gate_grad: float32 [1536, 4096], P(None, 'tensor')
- up_grad: float32 [1536, 4096], P(None, 'tensor')
- down_grad: float32 [4096, 1536], P('tensor')
Inputs may be any that keep to these rules, and one draw needn't show every extreme that they name: `segments`: each sequence holds exactly four documents, numbered from 0 on its first token, never falling and rising by one at the first token of each further document; one of the four is 256 tokens long and the others are shorter. `positions`: each token's position is its offset from the first token of its document in its sequence.
All inputs are finite; a program needn't handle non-finite values.
Results may differ from a plain program's by a relative error of at most 0.019.
Values may be sent and summed in bfloat16 or wider, within the bound.
A program may use at most 192 MiB of HBM per device.

v0:
```python
import math

import jax
import jax.numpy as jnp
from jax import lax
from jax.sharding import PartitionSpec as P

HEAD_SIZE = 96


EPS = 1e-05
THETA = 100000.0
NEG_LARGE = -1e30


def shifted(x, axis, by):
    peers = lax.axis_size(axis)
    pairs = [(i, i + by) for i in range(peers) if 0 <= i + by < peers]
    return lax.ppermute(x, axis, pairs)


def rope_tables(position_rows):
    steps_half = jnp.arange(HEAD_SIZE // 2).astype(jnp.float32)
    inverse = THETA ** (-2.0 * steps_half / HEAD_SIZE)
    angles = position_rows.astype(jnp.float32)[..., None] * inverse
    return (jnp.cos(angles), jnp.sin(angles))


def apply_rotary(operand, cosine, sine_part):
    half_width = operand.shape[-1] // 2
    lead_half = operand[..., :half_width]
    tail_half = operand[..., half_width:]
    return jnp.concatenate(
        [lead_half * cosine - tail_half * sine_part, tail_half * cosine + lead_half * sine_part],
        axis=-1,
    )


def inverse_rotary(operand, cosine, sine_part):
    half_width = operand.shape[-1] // 2
    lead_half = operand[..., :half_width]
    tail_half = operand[..., half_width:]
    return jnp.concatenate(
        [lead_half * cosine + tail_half * sine_part, tail_half * cosine - lead_half * sine_part],
        axis=-1,
    )


def dot_wide(left_side, right_side):
    return jnp.dot(left_side, right_side, preferred_element_type=jnp.float32)


def on_device(
    tokens,
    cotangent,
    segments,
    positions,
    norm_attn,
    w_query,
    key_weight,
    value_weight,
    w_out,
    norm_ffn,
    w_gate,
    w_up,
    w_down,
):
    single_float = jnp.float32
    brain_float_half = jnp.bfloat16
    seq_count, slice_len, model_width = tokens.shape
    seq_length = segments.shape[1]
    row_count = seq_count * slice_len
    query_width = w_query.shape[1]
    pair_width = key_weight.shape[1]
    kv_heads = pair_width // HEAD_SIZE
    group_of_head = query_width // HEAD_SIZE // kv_heads
    key_block = min(512, seq_length)
    score_scale = 1.0 / math.sqrt(HEAD_SIZE)
    my_slice = lax.axis_index("context")
    first_row = my_slice * slice_len
    query_seg = lax.dynamic_slice_in_dim(segments, first_row, slice_len, 1)
    query_index = first_row + jnp.arange(slice_len, dtype=jnp.int32)
    block_count = (first_row + slice_len + key_block - 1) // key_block
    tok_flat = tokens.reshape(row_count, model_width).astype(single_float)
    inv_attn = lax.rsqrt(jnp.mean(tok_flat * tok_flat, axis=-1, keepdims=True) + EPS)
    normalized_attention_input = (tok_flat * inv_attn * norm_attn.astype(single_float)).astype(
        brain_float_half
    )
    cosine, sine_part = rope_tables(positions)
    cos_query = cosine[:, :, None, None, :]
    sin_query = sine_part[:, :, None, None, :]
    cos_key = cosine[:, :, None, :]
    sin_key = sine_part[:, :, None, :]
    query_rows = apply_rotary(
        dot_wide(normalized_attention_input, w_query).reshape(
            seq_count, slice_len, kv_heads, group_of_head, HEAD_SIZE
        ),
        cos_query,
        sin_query,
    ).astype(brain_float_half)
    keys_local = apply_rotary(
        dot_wide(normalized_attention_input, key_weight).reshape(
            seq_count, slice_len, kv_heads, HEAD_SIZE
        ),
        cos_key,
        sin_key,
    ).astype(brain_float_half)
    values_local = dot_wide(normalized_attention_input, value_weight).astype(brain_float_half)
    pair_local = jnp.concatenate(
        [
            keys_local.reshape(seq_count, slice_len, pair_width),
            values_local.reshape(seq_count, slice_len, pair_width),
        ],
        axis=-1,
    )
    pair_all = lax.all_gather(pair_local, "context", axis=1, tiled=True)

    def score_block(pair_source, start_key):
        piece = lax.dynamic_slice_in_dim(pair_source, start_key, key_block, 1)
        key_part = piece[..., :pair_width].reshape(seq_count, key_block, kv_heads, HEAD_SIZE)
        value_part = piece[..., pair_width:].reshape(seq_count, key_block, kv_heads, HEAD_SIZE)
        scores = (
            jnp.einsum(
                "sigrd,sjgd->sgrij", query_rows, key_part, preferred_element_type=single_float
            )
            * score_scale
        )
        key_seg = lax.dynamic_slice_in_dim(segments, start_key, key_block, 1)
        key_index = start_key + jnp.arange(key_block, dtype=jnp.int32)
        allowed = (key_seg[:, None, :] == query_seg[:, :, None]) & (
            key_index[None, None, :] <= query_index[None, :, None]
        )
        return (scores, allowed[:, None, None, :, :], key_part, value_part)

    def stats_step(index_block, carry):
        run_max, run_sum = carry
        scores, allowed, key_part, value_part = score_block(pair_all, index_block * key_block)
        masked = jnp.where(allowed, scores, NEG_LARGE)
        new_max = jnp.maximum(run_max, jnp.max(masked, axis=-1))
        block_sum = jnp.sum(jnp.where(allowed, jnp.exp(masked - new_max[..., None]), 0.0), axis=-1)
        return (new_max, run_sum * jnp.exp(run_max - new_max) + block_sum)

    stat_shape = (seq_count, kv_heads, group_of_head, slice_len)
    run_max, run_sum = lax.fori_loop(
        0,
        block_count,
        stats_step,
        (jnp.full(stat_shape, NEG_LARGE, single_float), jnp.zeros(stat_shape, single_float)),
    )
    log_total = run_max + jnp.log(run_sum)

    def output_step(index_block, accum):
        scores, allowed, key_part, value_part = score_block(pair_all, index_block * key_block)
        probs = jnp.where(allowed, jnp.exp(scores - log_total[..., None]), 0.0).astype(
            brain_float_half
        )
        return accum + jnp.einsum(
            "sgrij,sjgd->sigrd", probs, value_part, preferred_element_type=single_float
        )

    attn_accum = lax.fori_loop(
        0,
        block_count,
        output_step,
        jnp.zeros((seq_count, slice_len, kv_heads, group_of_head, HEAD_SIZE), single_float),
    )
    attended = attn_accum.astype(brain_float_half).reshape(row_count, query_width)
    attn_total = lax.psum(dot_wide(attended, w_out).astype(jnp.bfloat16), "tensor").astype(
        jnp.float32
    )
    hidden_res = tok_flat + attn_total
    inv_ffn = lax.rsqrt(jnp.mean(hidden_res * hidden_res, axis=-1, keepdims=True) + EPS)
    normed_ffn = (hidden_res * inv_ffn * norm_ffn.astype(single_float)).astype(brain_float_half)
    gate_proj = dot_wide(normed_ffn, w_gate)
    up_proj = dot_wide(normed_ffn, w_up)
    sigmoid_gate = jax.nn.sigmoid(gate_proj)
    silu_gate = gate_proj * sigmoid_gate
    activated = (silu_gate * up_proj).astype(brain_float_half)
    ffn_total = lax.psum(dot_wide(activated, w_down).astype(jnp.bfloat16), "tensor").astype(
        jnp.float32
    )
    block_out = (
        (hidden_res + ffn_total).astype(brain_float_half).reshape(seq_count, slice_len, model_width)
    )
    grad_rows = cotangent.reshape(row_count, model_width)
    down_grad = dot_wide(activated.T, grad_rows)
    grad_act = dot_wide(grad_rows, w_down.T)
    grad_gate = (
        grad_act * up_proj * sigmoid_gate * (1.0 + gate_proj * (1.0 - sigmoid_gate))
    ).astype(brain_float_half)
    grad_up = (grad_act * silu_gate).astype(brain_float_half)
    gate_grad = dot_wide(normed_ffn.T, grad_gate)
    up_grad = dot_wide(normed_ffn.T, grad_up)
    grad_normed_ffn = lax.psum(
        (dot_wide(grad_gate, w_gate.T) + dot_wide(grad_up, w_up.T)).astype(jnp.bfloat16), "tensor"
    ).astype(jnp.float32)
    ffn_gain_grad = jnp.sum(grad_normed_ffn * hidden_res * inv_ffn, axis=0)
    scaled_ffn = grad_normed_ffn * norm_ffn.astype(single_float)
    grad_hidden = (
        grad_rows.astype(single_float)
        + inv_ffn * scaled_ffn
        - hidden_res * inv_ffn**3 * jnp.mean(scaled_ffn * hidden_res, axis=-1, keepdims=True)
    )
    grad_hidden_b = grad_hidden.astype(brain_float_half)
    out_grad = dot_wide(attended.T, grad_hidden_b)
    attended_gradient = (
        dot_wide(grad_hidden_b, w_out.T)
        .astype(brain_float_half)
        .reshape(seq_count, slice_len, kv_heads, group_of_head, HEAD_SIZE)
    )
    attended_heads = attended.reshape(seq_count, slice_len, kv_heads, group_of_head, HEAD_SIZE)
    row_delta = jnp.sum(
        attended_gradient.astype(single_float) * attended_heads.astype(single_float), axis=-1
    )
    delta_heads = jnp.transpose(row_delta, (0, 2, 3, 1))

    def grad_step(index_block, carry):
        query_accum, pair_accum = carry
        start_key = index_block * key_block
        scores, allowed, key_part, value_part = score_block(pair_all, start_key)
        weights = jnp.where(allowed, jnp.exp(scores - log_total[..., None]), 0.0)
        prob_grad = jnp.einsum(
            "sigrd,sjgd->sgrij", attended_gradient, value_part, preferred_element_type=single_float
        )
        score_grad = (weights * (prob_grad - delta_heads[..., None]) * score_scale).astype(
            brain_float_half
        )
        query_accum = query_accum + jnp.einsum(
            "sgrij,sjgd->sigrd", score_grad, key_part, preferred_element_type=single_float
        )
        key_term = jnp.einsum(
            "sgrij,sigrd->sjgd", score_grad, query_rows, preferred_element_type=single_float
        )
        value_term = jnp.einsum(
            "sgrij,sigrd->sjgd",
            weights.astype(brain_float_half),
            attended_gradient,
            preferred_element_type=single_float,
        )
        both_terms = jnp.concatenate(
            [
                key_term.reshape(seq_count, key_block, pair_width),
                value_term.reshape(seq_count, key_block, pair_width),
            ],
            axis=-1,
        )
        current = lax.dynamic_slice_in_dim(pair_accum, start_key, key_block, 1)
        pair_accum = lax.dynamic_update_slice_in_dim(pair_accum, current + both_terms, start_key, 1)
        return (query_accum, pair_accum)

    query_accum, pair_accum = lax.fori_loop(
        0,
        block_count,
        grad_step,
        (
            jnp.zeros((seq_count, slice_len, kv_heads, group_of_head, HEAD_SIZE), single_float),
            jnp.zeros((seq_count, seq_length, 2 * pair_width), single_float),
        ),
    )
    slice_count = lax.axis_size("context")

    def owner_step(turn, incoming):
        owner = my_slice + turn - (slice_count - 1)
        own_rows = lax.dynamic_slice_in_dim(
            pair_accum, jnp.maximum(owner, 0) * slice_len, slice_len, 1
        )
        message = jnp.where(owner >= 0, incoming + own_rows, 0.0)
        return shifted(message, "context", -1)

    arrived = lax.fori_loop(
        0,
        slice_count - 1,
        owner_step,
        jnp.zeros((seq_count, slice_len, 2 * pair_width), single_float),
    )
    pair_grad = arrived + lax.dynamic_slice_in_dim(pair_accum, first_row, slice_len, 1)
    key_linear = (
        inverse_rotary(
            pair_grad[..., :pair_width].reshape(seq_count, slice_len, kv_heads, HEAD_SIZE),
            cos_key,
            sin_key,
        )
        .astype(brain_float_half)
        .reshape(row_count, pair_width)
    )
    value_linear = (
        pair_grad[..., pair_width:].astype(brain_float_half).reshape(row_count, pair_width)
    )
    query_lin = (
        inverse_rotary(query_accum, cos_query, sin_query)
        .astype(brain_float_half)
        .reshape(row_count, query_width)
    )
    query_grad = dot_wide(normalized_attention_input.T, query_lin)
    key_grad = dot_wide(normalized_attention_input.T, key_linear)
    value_grad = dot_wide(normalized_attention_input.T, value_linear)
    back_attn = (
        dot_wide(query_lin, w_query.T)
        + dot_wide(key_linear, key_weight.T)
        + dot_wide(value_linear, value_weight.T)
    )
    grad_normed_attn = lax.psum(back_attn.astype(jnp.bfloat16), "tensor").astype(jnp.float32)
    attn_gain_grad = jnp.sum(grad_normed_attn * tok_flat * inv_attn, axis=0)
    scaled_attn = grad_normed_attn * norm_attn.astype(single_float)
    input_grad = (
        grad_hidden
        + inv_attn * scaled_attn
        - tok_flat * inv_attn**3 * jnp.mean(scaled_attn * tok_flat, axis=-1, keepdims=True)
    )
    input_grad = input_grad.astype(brain_float_half).reshape(seq_count, slice_len, model_width)
    all_sums = lax.psum(
        (
            attn_gain_grad,
            query_grad,
            key_grad,
            value_grad,
            out_grad,
            ffn_gain_grad,
            gate_grad,
            up_grad,
            down_grad,
        ),
        ("dp", "context"),
    )
    return (
        block_out,
        input_grad,
        all_sums[0],
        all_sums[1],
        all_sums[2],
        all_sums[3],
        all_sums[4],
        all_sums[5],
        all_sums[6],
        all_sums[7],
        all_sums[8],
    )


def solution(mesh):
    placed = (
        P("dp", "context", None),
        P("dp", "context", None),
        P("dp", None),
        P("dp", "context"),
        P(),
        P(None, "tensor"),
        P(None, "tensor"),
        P(None, "tensor"),
        P("tensor", None),
        P(),
        P(None, "tensor"),
        P(None, "tensor"),
        P("tensor", None),
    )
    return jax.shard_map(
        on_device,
        mesh=mesh,
        in_specs=placed,
        out_specs=(
            P("dp", "context", None),
            P("dp", "context", None),
            P(),
            P(None, "tensor"),
            P(None, "tensor"),
            P(None, "tensor"),
            P("tensor", None),
            P(),
            P(None, "tensor"),
            P(None, "tensor"),
            P("tensor", None),
        ),
        check_vma=False,
    )
```

profile of v0, /device:TPU:0, one launch (start us, length us, event | category | flops | bytes accessed | tf_op | source)
XLA Modules:
  0.0 890.2 jit_solution(11171474708792457560)
XLA Ops:
  8.1 2.3 fusion.50
  10.4 2.3 fusion.52
  16.5 1.6 convolution_convert_fusion.3
  18.2 1.8 reshape.331
  20.0 2.5 pad_maximum_fusion
  22.6 2.4 copy.51
  25.0 3.1 fusion.57
  29.1 23.4 %all-gather.2.cloned.1.call-done = bf16[3,512,384]{1,0,2:T(4,128)(2,1)} async-done(((bf16[3,256,384]{1,0,2:T(4,128)(2,1)}), bf16[3,512,384]{1,0,2:T(4,128)(2,1)}) %all-gather.2.cloned.1.call-update) | async-done | bytes 1179664 | tf_op jit(solution)/shard_map/all_gather | solution.py:116
  52.6 2.7 copy.53
  55.3 5.6 while.42
  56.9 2.3 fusion.157
  59.3 1.6 select_reduce_fusion.2
  62.6 8.1 while.43
  63.1 2.4 fusion.162
  65.5 4.7 fusion.163
  70.7 3.3 copy.54
  74.0 3.3 reshape.332
  77.2 4.2 convolution_convert_fusion.1
  82.2 94.1 %all-reduce.8.cloned.1.call-done = bf16[768,1536]{1,0:T(8,128)(2,1)} async-done(((bf16[768,1536]{1,0:T(8,128)(2,1)}), bf16[768,1536]{1,0:T(8,128)(2,1)}) %all-reduce.8.cloned.1.call-update) | async-done | bytes 2359312 | tf_op jit(solution)/shard_map/psum | solution.py:168
  176.3 3.4 multiply_reduce_fusion
  182.0 2.6 fusion.70
  184.7 2.6 fusion.69
  187.3 5.0 multiply_convert_fusion.1
  192.3 2.6 fusion.71
  195.0 4.0 add_convert_fusion.1
  199.2 93.6 %all-reduce.10.cloned.1.call-done = bf16[768,1536]{1,0:T(8,128)(2,1)} async-done(((bf16[768,1536]{1,0:T(8,128)(2,1)}), bf16[768,1536]{1,0:T(8,128)(2,1)}) %all-reduce.10.cloned.1.call-update) | async-done | bytes 2359312 | tf_op jit(solution)/shard_map/psum | solution.py:194
  292.8 5.0 fusion.47
  297.9 3.5 fusion.44
  301.5 2.1 copy-done.8
  303.6 2.2 convolution_convert_fusion.2
  305.8 3.7 reshape.335
  309.5 4.4 multiply_reduce_fusion.1
  313.9 3.0 copy.56
  319.3 1.7 broadcast_in_dim.84
  321.0 12.0 %while.44 = (s32[]{:T(128)}, f32[3,256,2,2,96]{1,4,3,2,0:T(8,128)}, f32[3,512,384]{1,2,0:T(8,128)}, s32[]{:T(128)}, s32[3,512]{1,0:T(4,128)S(1)}, /*index=5*/s32...) while((s32[]{:T(128)}, f32[3,256,2,2,96]{1,4,3,2,0:T(8,128)}, ...), condition=%wide.region_14.15_spmd.clone, body=%wide.region_13.14_spmd.clone.sunk | while | flops 1529643776 | bytes 81120576 | solution.py:251
  324.2 1.4 fusion.178
  325.7 2.5 fusion.176
  331.7 1.4 copy-done.6
  333.1 2.5 dynamic-slice_select_fusion
  336.9 3.8 convolution_convert_fusion
  341.8 3.0 copy.58
  344.8 3.3 convert_element_type.180
  348.1 3.0 fusion.72
  351.1 14.2 %collective-permute-done = f32[3,256,384]{1,2,0:T(8,128)} collective-permute-done((f32[3,256,384]{1,2,0:T(8,128)}, f32[3,256,384]{1,2,0:T(8,128)}, u32[]{:S(2)}, u32[]{:S(2)}) %collective-permute-start) | collective-permute-done | bytes 1179680 | tf_op jit(solution)/shard_map/while/body/eval_jaxpr/ppermute | solution.py:19
  365.3 1.5 dynamic-slice_add_fusion
  369.4 2.2 add_convert_fusion
  372.0 7.6 fusion.77
  379.6 4.6 fusion.76
  384.2 4.6 fusion.75
  388.8 2.8 fusion.74
  391.7 2.6 fusion.61
  394.2 1.6 convolution_bitcast_fusion.1
  395.9 1.6 fusion.78
  398.2 143.9 %all-reduce.14.cloned.1.call-done = (bf16[768,1536]{1,0:T(8,128)(2,1)}, bf16[768,1536]{1,0:T(8,128)(2,1)}) async-done(((bf16[768,1536]{1,0:T(8,128)(2,1)}, bf16[768,1536]{1,0:T(8,128)(2,1)}), (bf16[768,1536]{1,0:T(8,128)(2,1)}, bf16[768,1536]{1,0:T(8,128)(2,1)})) %all-reduce.14.cloned.1.call-update) | async-done | bytes 4718608 | tf_op jit(solution)/shard_map/psum | solution.py:179
  542.1 4.1 fusion.49
  546.2 25.9 %all-reduce = (f32[1536]{0:T(1024)}, f32[1536]{0:T(1024)}) all-reduce(f32[1536]{0:T(1024)S(1)} %get-tuple-element.347, f32[1536]{0:T(1024)S(1)} %get-tuple-element.345), channel_id=1, replica_groups=mesh['dp'=4,'context'=2,'tensor'=4] {'dp','context'}, use_global_device_ids=true, to_apply=%region_18.19 | all-reduce | flops 3072 | bytes 24576 | tf_op jit(solution)/shard_map/psum | solution.py:311
  572.1 8.9 %fusion.41 = (bf16[768,1536]{1,0:T(8,128)(2,1)}, bf16[768,1536]{1,0:T(8,128)(2,1)}) fusion(f32[768,1536]{1,0:T(8,128)} %copy-done.8, bf16[768,1536]{1,0:T(8,128)(2,1)} %get-tuple-element.419, bf16[3,256,1536]{2,1,0:T(8,128)(2,1)} %param.19, f32[768]{0:T(1024)S(1)} %broadcast_multiply_fusion, f32[768]{0:T(1024)S(1)} %multiply_multiply_fusion, ...), kind=kLoop, calls=%fused_computation.55 | loop fusion | flops 16515072 | bytes 18889728 | tf_op jit(solution)/shard_map/convert_element_type | solution.py:310
  581.0 282.7 %all-reduce.12.cloned.1.call-done = (f32[1536,384]{1,0:T(8,128)}, f32[1536,192]{0,1:T(8,128)}, f32[1536,192]{0,1:T(8,128)}, f32[384,1536]{1,0:T(8,128)}, f32[153...) async-done(((f32[1536,384]{1,0:T(8,128)}, f32[1536,192]{0,1:T(8,128)}, f32[1536,192]{0,1:T(8,128)}, f32[384,1536]{1,0:T(8,128)}, f32[1536,1024]{1,0:T(8,128)}, ...) | async-done | bytes 25952272 | tf_op jit(solution)/shard_map/psum | solution.py:311
  863.7 3.4 copy.112
  869.4 1.4 copy.115
  870.8 1.6 copy-done.17
  872.4 3.2 copy.116
  875.9 3.2 copy.117
  880.5 2.7 copy.118
  (188 shorter events, 31.9 us)
Async XLA Ops:
  7.2 180.2 %copy-start = (bf16[1024,1536]{1,0:T(8,128)(2,1)S(1)}, bf16[1024,1536]{1,0:T(8,128)(2,1)}, u32[]{:S(2)}) copy-start(bf16[1024,1536]{1,0:T(8,128)(2,1)} %param.31) | copy-start | bytes 9437188
  7.2 3.2 copy-start.44
  7.2 45.4 %all-gather.2.cloned.1.call-start = ((), (), s32[]{:S(2)}) async-start(), calls=%async_computation | async-start | bytes 2359296 | tf_op jit(solution)/shard_map/all_gather | solution.py:116
  10.4 5.1 copy-start.41
  10.4 5.1 copy-start.39
  10.4 3.0 copy-start.26
  12.8 1.7 copy-start.14
  13.4 14.7 %copy-start.21 = (f32[3,256,48]{1,2,0:T(8,128)}, f32[3,256,48]{1,2,0:T(8,128)S(1)}, u32[]{:S(2)}) copy-start(f32[3,256,48]{1,2,0:T(8,128)S(1)} %get-tuple-element.439) | copy-start | bytes 442372
  13.4 14.7 %copy-start.23 = (f32[3,256,48]{1,2,0:T(8,128)}, f32[3,256,48]{1,2,0:T(8,128)S(1)}, u32[]{:S(2)}) copy-start(f32[3,256,48]{1,2,0:T(8,128)S(1)} %get-tuple-element.440) | copy-start | bytes 442372
  13.4 2.1 copy-start.1
  15.5 1.1 copy-start.36
  20.0 5.0 copy-start.32
  22.5 153.8 %all-reduce.8.cloned.1.call-start = ((), (), s32[]{:S(2)}) async-start(), calls=%async_computation.1 | async-start | bytes 4718592 | tf_op jit(solution)/shard_map/psum | solution.py:168
  81.5 0.7 copy-start.45
  81.5 211.2 %all-reduce.10.cloned.1.call-start = ((), (), s32[]{:S(2)}) async-start(), calls=%async_computation.2 | async-start | bytes 4718592 | tf_op jit(solution)/shard_map/psum | solution.py:194
  176.3 3.4 copy-start.2
  176.3 3.8 copy-start.9
  180.1 1.9 copy-start.47
  182.0 2.6 copy-start.30
  182.0 2.7 copy-start.46
  184.7 2.6 copy-start.28
  192.3 2.6 copy-start.49
  192.3 2.7 copy-start.51
  198.9 343.2 %all-reduce.14.cloned.1.call-start = ((), (), s32[]{:S(2)}) async-start(), calls=%async_computation.4 | async-start | bytes 9437184 | tf_op jit(solution)/shard_map/psum | solution.py:179
  292.8 5.0 copy-start.3
  292.8 5.0 copy-start.10
  292.8 5.2 copy-start.16
  297.9 5.7 copy-start.33
  301.5 2.1 copy-start.8
  316.9 4.2 copy-start.43
  321.2 1.9 copy-start.4
  323.2 1.1 copy-start.38
  325.7 2.5 copy-start.11
  329.0 1.1 copy-start.12
  329.0 2.1 copy-start.5
  331.7 1.4 copy-start.6
  333.1 3.8 copy-start.48
  335.6 29.7 %collective-permute-start = (f32[3,256,384]{1,2,0:T(8,128)}, f32[3,256,384]{1,2,0:T(8,128)}, u32[]{:S(2)}, u32[]{:S(2)}) collective-permute-start(f32[3,256,384]{1,2,0:T(8,128)} %dynamic-slice_select_fusion), channel_id=1, source_target_pairs={{4,0},{5,1},{6,2},{7,3},{12,8},{13,9},{14,10},{15,11},{20,16},{21,... | collective-permute-start | bytes 3538952 | tf_op jit(solution)/shard_map/while/body/eval_jaxpr/ppermute | solution.py:19
  336.9 3.9 copy-start.13
  336.9 3.9 copy-start.22
  336.9 3.8 copy-start.24
  348.1 17.3 %copy-start.7 = (f32[3,512,384]{1,2,0:T(8,128)S(1)}, f32[3,512,384]{1,2,0:T(8,128)}, u32[]{:S(2)}) copy-start(f32[3,512,384]{1,2,0:T(8,128)} %get-tuple-element.191) | copy-start | bytes 7077892
  366.8 1.0 copy-start.18
  366.9 1.5 copy-start.27
  368.3 1.1 copy-start.37
  371.6 492.1 %all-reduce.12.cloned.1.call-start = ((), (), s32[]{:S(2)}) async-start(), calls=%async_computation.3 | async-start | bytes 51904512 | tf_op jit(solution)/shard_map/psum | solution.py:311
  371.9 7.7 copy-start.31
  372.0 7.7 copy-start.52
  379.6 4.6 copy-start.50
  379.6 12.0 %slice-start = ((s8[4718592]{0:T(1024)(128)(4,1)}), s8[4194304]{0:T(1024)(128)(4,1)S(1)}, s32[]{:S(2)}) async-start(s8[4718592]{0:T(1024)(128)(4,1)} %bitcast.261), calls=%async_computation.5 | async-start | bytes 8388608
  384.2 4.6 copy-start.15
  384.2 4.6 copy-start.20
  384.2 7.4 slice-start.1
  388.8 2.8 copy-start.25
  391.7 2.6 copy-start.19
  397.5 144.6 %copy-start.40 = (f32[1536]{0:T(1024)S(1)}, f32[1536]{0:T(1024)}, u32[]{:S(2)}) copy-start(f32[1536]{0:T(1024)} %copy-done.39) | copy-start | bytes 18436
  863.7 3.4 copy-start.35
  863.7 4.4 copy-start.34
  867.1 2.3 copy-start.29
  868.1 4.3 copy-start.17
  869.4 6.2 slice-start.4
  872.4 3.4 slice-start.5
  872.4 7.0 slice-start.2
  875.9 4.6 slice-start.3
  (1 other events, 0.7 us)
Sparse Core Ops, SparseCore 0:
  22.7 29.8 all-gather.1
  81.6 94.6 all-reduce.7
  199.1 93.6 all-reduce.9
  371.8 170.3 all-reduce.13
  548.3 315.3 all-reduce.11
where the time goes:
time: 899 us; the launch traced here: 890 us
  waiting for transfers between devices  652 us (73%)
  matrix products  78 us (9%)
  local copies, waits for them, and re-layouts  66.8 us (7%)
  other arithmetic  49.9 us (6%)
  blocking collectives  25.9 us (3%)
  between operations  14.8 us (2%)
    psum x1, waiting for transfers between devices, on_device(): lax.psum((attn_gain_grad, query_grad, key_grad, value_grad, out_grad, ffn...  283 us
    psum x1, waiting for transfers between devices, on_device(): lax.psum(dot_wide(activated, w_down).astype(jnp.bfloat16), 'tensor')  144 us
    psum x1, waiting for transfers between devices, on_device(): lax.psum(dot_wide(attended, w_out).astype(jnp.bfloat16), 'tensor')  94.1 us
    psum x1, waiting for transfers between devices, on_device(): lax.psum((dot_wide(grad_gate, w_gate.T) + dot_wide(grad_up, w_up.T)).asty...  93.6 us
    dot_general x21, matrix products, dot_wide(): return jnp.dot(left_side, right_side, preferred_element_type=jnp.float32)  64.1 us
    unnamed x119, local copies, waits for them, and re-layouts  35.9 us
    psum x1, blocking collectives, on_device(): lax.psum((attn_gain_grad, query_grad, key_grad, value_grad, out_grad, ffn...  25.9 us
    all_gather x1, waiting for transfers between devices, on_device(): pair_all = lax.all_gather(pair_local, 'context', axis=1, tiled=True)  23.4 us
  transfers between devices with their start and end apart: 6, of which 6 were waited for; matrix products, arithmetic and copies ran while one was open for 7% of the time, Pallas kernels for 0%

commit v1 on v0

v1 whole, which is shorter than its diff:
```python
import functools
import math

import jax
import jax.numpy as jnp
from jax import lax
from jax.experimental import pallas as pl
from jax.experimental.pallas import tpu as pltpu
from jax.sharding import PartitionSpec as P

HEAD = 96
PAD = 128
EPS = 1e-05
THETA = 100000.0
NEG = -1e30
F32 = jnp.float32
BF16 = jnp.bfloat16
MESH = pl.DeviceIdType.MESH
VMEM = pltpu.MemorySpace.VMEM
HALVES = 2


def mm(a, b):
    return jnp.dot(a, b, preferred_element_type=F32)


def mm_nt(a, b):
    return lax.dot_general(a, b, (((1,), (1,)), ((), ())), preferred_element_type=F32)


def mm_tn(a, b):
    return lax.dot_general(a, b, (((0,), (0,)), ((), ())), preferred_element_type=F32)


class Line:
    def __init__(self, axis, part, rbuf, full, rs_send, rs_recv, ag_send, ag_recv):
        self.axis = axis
        self.n = lax.axis_size(axis)
        self.me = lax.axis_index(axis)
        self.part, self.rbuf, self.full = part, rbuf, full
        self.rs_send, self.rs_recv = rs_send, rs_recv
        self.ag_send, self.ag_recv = ag_send, ag_recv

    def rs_copy(self, u, side, j):
        n = self.n
        slot = j - 1 if side == 0 else j
        return pltpu.make_async_remote_copy(
            src_ref=self.part.at[u, j],
            dst_ref=self.rbuf.at[u, side, slot],
            send_sem=self.rs_send.at[u, side, slot],
            recv_sem=self.rs_recv.at[u, side, slot],
            device_id={self.axis: self.me + (1 if side == 0 else -1)},
            device_id_type=MESH,
        )

    def rs_start(self, u):
        n, me = self.n, self.me

        @pl.when(me == 0)
        def _():
            for j in range(n - 1, 0, -1):
                self.rs_copy(u, 0, j).start()

        @pl.when(me == n - 1)
        def _():
            for j in range(n - 1):
                self.rs_copy(u, 1, j).start()

    def rs_step(self, u, t):
        n, me = self.n, self.me
        j = n - 1 - t

        @pl.when((me > 0) & (me <= j))
        def _():
            self.rs_copy(u, 0, j).wait_recv()

        @pl.when((me > 0) & (me < j))
        def _():
            self.part[u, j] = (
                self.part[u, j].astype(F32) + self.rbuf[u, 0, j - 1].astype(F32)
            ).astype(BF16)
            self.rs_copy(u, 0, j).start()

        k = t

        @pl.when((me < n - 1) & (me >= k))
        def _():
            self.rs_copy(u, 1, k).wait_recv()

        @pl.when((me < n - 1) & (me > k))
        def _():
            self.part[u, k] = (
                self.part[u, k].astype(F32) + self.rbuf[u, 1, k].astype(F32)
            ).astype(BF16)
            self.rs_copy(u, 1, k).start()

    def rs_own(self, u, out):
        n, me = self.n, self.me
        out[...] = self.part[u, me].astype(F32)

        @pl.when(me > 0)
        def _():
            out[...] += self.rbuf[u, 0, me - 1].astype(F32)

        @pl.when(me < n - 1)
        def _():
            out[...] += self.rbuf[u, 1, me].astype(F32)

    def rs_drain(self, u):
        n, me = self.n, self.me
        for j in range(1, n):

            @pl.when(me < j)
            def _():
                self.rs_copy(u, 0, j).wait_send()

        for j in range(n - 1):

            @pl.when(me > j)
            def _():
                self.rs_copy(u, 1, j).wait_send()

    def ag_copy(self, u, side, j):
        return pltpu.make_async_remote_copy(
            src_ref=self.full.at[u, j],
            dst_ref=self.full.at[u, j],
            send_sem=self.ag_send.at[u, side, j],
            recv_sem=self.ag_recv.at[u, side, j],
            device_id={self.axis: self.me + (1 if side == 0 else -1)},
            device_id_type=MESH,
        )

    def ag_start(self, u):
        n, me = self.n, self.me

        @pl.when(me < n - 1)
        def _():
            self.ag_copy(u, 0, me).start()

        @pl.when(me > 0)
        def _():
            self.ag_copy(u, 1, me).start()

    def ag_step(self, u, s):
        n, me = self.n, self.me

        @pl.when(me - s >= 0)
        def _():
            self.ag_copy(u, 0, me - s).wait_recv()

        @pl.when((me - s >= 0) & (me < n - 1))
        def _():
            self.ag_copy(u, 0, me - s).start()

        @pl.when(me + s <= n - 1)
        def _():
            self.ag_copy(u, 1, me + s).wait_recv()

        @pl.when((me + s <= n - 1) & (me > 0))
        def _():
            self.ag_copy(u, 1, me + s).start()

    def ag_drain(self, u):
        n, me = self.n, self.me
        for j in range(n):

            @pl.when((j <= me) & (me < n - 1))
            def _():
                self.ag_copy(u, 0, j).wait_send()

            @pl.when((j >= me) & (me > 0))
            def _():
                self.ag_copy(u, 1, j).wait_send()


def line_sems(units, n):
    return [
        pltpu.SemaphoreType.DMA((units, 2, n - 1)),
        pltpu.SemaphoreType.DMA((units, 2, n - 1)),
        pltpu.SemaphoreType.DMA((units, 2, n)),
        pltpu.SemaphoreType.DMA((units, 2, n)),
    ]


def enter(context_peers):
    n, me = lax.axis_size("tensor"), lax.axis_index("tensor")
    slices, mine = lax.axis_size("context"), lax.axis_index("context")
    barrier = pltpu.get_barrier_semaphore()

    @pl.when(me > 0)
    def _():
        pl.semaphore_signal(barrier, inc=1, device_id={"tensor": me - 1}, device_id_type=MESH)

    @pl.when(me < n - 1)
    def _():
        pl.semaphore_signal(barrier, inc=1, device_id={"tensor": me + 1}, device_id_type=MESH)

    for d in range(1, slices):

        @pl.when(mine + d < slices)
        def _():
            pl.semaphore_signal(
                barrier, inc=1, device_id={"context": mine + d}, device_id_type=MESH
            )

        @pl.when(mine - d >= 0)
        def _():
            pl.semaphore_signal(
                barrier, inc=1, device_id={"context": mine - d}, device_id_type=MESH
            )

    @pl.when((me > 0) & (me < n - 1))
    def _():
        pl.semaphore_wait(barrier, slices + 1)

    @pl.when((me == 0) | (me == n - 1))
    def _():
        pl.semaphore_wait(barrier, slices)


def lane_of(shape):
    return lax.broadcasted_iota(jnp.int32, shape, len(shape) - 1)


def swap_halves(x):
    width = x.shape[-1]
    half = HEAD // 2
    first = (lane_of(x.shape) % HEAD) < half
    return jnp.where(first, pltpu.roll(x, width - half, 1), pltpu.roll(x, half, 1))


def take_head(x, h):
    width = x.shape[-1]
    moved = x if h == 0 else pltpu.roll(x, width - h * HEAD, 1)
    moved = moved[:, :PAD]
    return jnp.where(lane_of(moved.shape) < HEAD, moved, 0.0)


def put_heads(pieces, width):
    rows = pieces[0].shape[0]
    total = None
    for h, piece in enumerate(pieces):
        wide = jnp.concatenate([piece, jnp.zeros((rows, width - PAD), F32)], axis=1)
        wide = wide if h == 0 else pltpu.roll(wide, h * HEAD, 1)
        total = wide if total is None else total + wide
    return total


def mask_of(qseg, kseg, diagonal):
    ok = qseg == kseg
    if diagonal:
        shape = ok.shape
        ok = ok & (
            lax.broadcasted_iota(jnp.int32, shape, 1) <= lax.broadcasted_iota(jnp.int32, shape, 0)
        )
    return ok


def twice(ok):
    bias = jnp.where(ok, 0.0, NEG)
    return jnp.concatenate([bias, bias], axis=0)


def forward_kernel(
    seqs,
    tokens,
    cot,
    qseg,
    kseg,
    na,
    nf,
    wqkv,
    w_out,
    w_gate,
    w_up,
    w_down,
    cos,
    sin,
    normed_attn,
    qpad,
    kv,
    lse,
    attended,
    attpad,
    hidden_own,
    normed_ffn,
    act,
    ggate,
    gup,
    ffn_part,
    gh_own,
    ghb,
    ffn_gain,
    part_a,
    rbuf_a,
    part_c,
    rbuf_c,
    gact,
    own,
    a_rs_s,
    a_rs_r,
    a_ag_s,
    a_ag_r,
    c_rs_s,
    c_rs_r,
    c_ag_s,
    c_ag_r,
    kv_s,
    kv_r,
):
    n = lax.axis_size("tensor")
    me = lax.axis_index("tensor")
    slices, mine = lax.axis_size("context"), lax.axis_index("context")
    rows = tokens.shape[0] // seqs
    width = tokens.shape[1]
    qw = w_out.shape[0]
    heads = qw // HEAD
    kvh = heads // 2
    pairw = wqkv.shape[1] - qw
    hidden = w_gate.shape[1]
    shard = rows // HALVES // n
    scale = 1.0 / math.sqrt(HEAD)
    line_a = Line("tensor", part_a, rbuf_a, normed_ffn, a_rs_s, a_rs_r, a_ag_s, a_ag_r)
    line_c = Line("tensor", part_c, rbuf_c, ghb, c_rs_s, c_rs_r, c_ag_s, c_ag_r)
    enter(True)

    def rows_of(c):
        return pl.ds(c * rows, rows)

    def kv_copy(c, d):
        return pltpu.make_async_remote_copy(
            src_ref=kv.at[c, mine],
            dst_ref=kv.at[c, mine],
            send_sem=kv_s.at[c, d - 1],
            recv_sem=kv_r.at[c, d - 1],
            device_id={"context": mine + d},
            device_id_type=MESH,
        )

    def project(c):
        x = tokens[rows_of(c), :].astype(F32)
        inv = lax.rsqrt(jnp.mean(x * x, axis=-1, keepdims=True) + EPS)
        normed = (x * inv * na[...]).astype(BF16)
        normed_attn[rows_of(c), :] = normed
        ct, st = cos[rows_of(c), :], sin[rows_of(c), :]
        q = mm(normed, wqkv[:, :qw])
        q = q * ct + swap_halves(q) * st
        for h in range(heads):
            qpad[c, h] = take_head(q, h).astype(BF16)
        p = mm(normed, wqkv[:, qw:])
        roped = p * ct[:, :pairw] + swap_halves(p) * st[:, :pairw]
        p = jnp.where(lane_of(p.shape) < kvh * HEAD, roped, p)
        for h in range(2 * kvh):
            kv[c, mine, h] = take_head(p, h).astype(BF16)
        for d in range(1, slices):

            @pl.when(mine + d < slices)
            def _():
                kv_copy(c, d).start()

    def attend(c):
        for d in range(1, slices):

            @pl.when(mine - d >= 0)
            def _():
                pltpu.make_async_remote_copy(
                    src_ref=kv.at[c, mine - d],
                    dst_ref=kv.at[c, mine - d],
                    send_sem=kv_s.at[c, d - 1],
                    recv_sem=kv_r.at[c, d - 1],
                    device_id={"context": mine - d},
                    device_id_type=MESH,
                ).wait_recv()

        qs = qseg[c]
        outs = []
        bias0 = twice(mask_of(qs, kseg[c, mine], True))
        for g in range(kvh):
            q2 = qpad[c, 2 * g : 2 * g + 2].reshape(2 * rows, PAD)
            s = mm_nt(q2, kv[c, mine, g]) * scale + bias0
            m = jnp.max(s, axis=-1, keepdims=True)
            p = jnp.exp(s - m)
            l = jnp.sum(p, axis=-1, keepdims=True)
            acc = mm(p.astype(BF16), kv[c, mine, kvh + g])

            def block(b, carry):
                m, l, acc = carry
                bias = twice(mask_of(qs, kseg[c, b], False))
                s = mm_nt(q2, kv[c, b, g]) * scale + bias
                m2 = jnp.maximum(m, jnp.max(s, axis=-1, keepdims=True))
                alpha = jnp.exp(m - m2)
                p = jnp.exp(s - m2)
                return (
                    m2,
                    l * alpha + jnp.sum(p, axis=-1, keepdims=True),
                    acc * alpha + mm(p.astype(BF16), kv[c, b, kvh + g]),
                )

            m, l, acc = lax.fori_loop(0, mine, block, (m, l, acc))
            lse[c, g] = m + jnp.log(l)
            out = acc / l
            outs += [out[:rows], out[rows:]]
        for h in range(heads):
            attpad[c, h] = outs[h].astype(BF16)
        attended[rows_of(c), :] = put_heads(outs, qw).astype(BF16)

    def units(c):
        return range(c * HALVES, (c + 1) * HALVES)

    def store_part(part, c, col, wide, value):
        part[pl.ds(c * HALVES, HALVES), :, :, pl.ds(col, wide)] = value.astype(BF16).reshape(
            HALVES, n, shard, wide
        )

    step = 512

    def out_project(c):
        a = attended[rows_of(c), :]
        for t in range(0, width, step):
            store_part(part_a, c, t, step, mm(a, w_out[:, t : t + step]))
        for u in units(c):
            line_a.rs_start(u)

    def a_reduce(c):
        for t in range(n - 1):
            for u in units(c):
                line_a.rs_step(u, t)
        for u in units(c):
            line_a.rs_own(u, own)
            start = pl.multiple_of(u * n * shard + me * shard, shard)
            hid = own[...] + tokens[pl.ds(start, shard), :].astype(F32)
            hidden_own[u] = hid
            inv = lax.rsqrt(jnp.mean(hid * hid, axis=-1, keepdims=True) + EPS)
            normed_ffn[u, me] = (hid * inv * nf[...]).astype(BF16)
            line_a.ag_start(u)

    def a_gather(c, s):
        for u in units(c):
            line_a.ag_step(u, s)

    def cot_back(c):
        k = cot[rows_of(c), :]
        for t in range(0, hidden, step):
            gact[rows_of(c), t : t + step] = mm_nt(k, w_down[t : t + step, :])

    def ffn(c):
        x = normed_ffn[pl.ds(c * HALVES, HALVES)].reshape(rows, width)
        tile = 256

        def body(i, _):
            cols = pl.ds(pl.multiple_of(i * tile, tile), tile)
            gp = mm(x, w_gate[:, cols])
            up = mm(x, w_up[:, cols])
            ga = gact[rows_of(c), cols]
            sig = jax.nn.sigmoid(gp)
            silu = gp * sig
            act[rows_of(c), cols] = (silu * up).astype(BF16)
            ggate[rows_of(c), cols] = (ga * up * sig * (1.0 + gp * (1.0 - sig))).astype(BF16)
            gup[rows_of(c), cols] = (ga * silu).astype(BF16)
            return 0

        lax.fori_loop(0, hidden // tile, body, 0)

    def ffn_back(c):
        gg, gu = ggate[rows_of(c), :], gup[rows_of(c), :]
        for t in range(0, width, step):
            store_part(
                part_c,
                c,
                t,
                step,
                mm_nt(gg, w_gate[t : t + step, :]) + mm_nt(gu, w_up[t : t + step, :]),
            )
        for u in units(c):
            line_c.rs_start(u)

    def ffn_out(c):
        a = act[rows_of(c), :]
        for t in range(0, width, step):
            store_part(ffn_part, c, t, step, mm(a, w_down[:, t : t + step]))

    def c_reduce(c):
        for t in range(n - 1):
            for u in units(c):
                line_c.rs_step(u, t)
        for u in units(c):
            line_c.rs_own(u, own)
            g = own[...]
            hid = hidden_own[u]
            start = pl.multiple_of(u * n * shard + me * shard, shard)
            inv = lax.rsqrt(jnp.mean(hid * hid, axis=-1, keepdims=True) + EPS)
            ffn_gain[...] += jnp.sum(g * hid * inv, axis=0, keepdims=True)
            scaled = g * nf[...]
            gh = (
                cot[pl.ds(start, shard), :].astype(F32)
                + inv * scaled
                - hid * (inv * inv * inv) * jnp.mean(scaled * hid, axis=-1, keepdims=True)
            )
            gh_own[u] = gh
            ghb[u, me] = gh.astype(BF16)
            line_c.ag_start(u)

    def c_gather(c, s):
        for u in units(c):
            line_c.ag_step(u, s)

    ffn_gain[...] = jnp.zeros_like(ffn_gain)
    for c in range(seqs):
        project(c)
    for c in range(seqs):
        attend(c)
        out_project(c)
        if c >= 1:
            a_reduce(c - 1)
        if c >= 2:
            for s in range(1, n):
                a_gather(c - 2, s)
    for c in range(seqs):
        cot_back(c)
        if c == 0:
            a_reduce(seqs - 1)
            if seqs >= 2:
                a_gather(seqs - 2, 1)
        elif seqs >= 2 and c + 1 < n:
            a_gather(seqs - 2, c + 1)
    if seqs >= 2:
        for s in range(seqs + 1, n):
            a_gather(seqs - 2, s)
    for c in range(seqs):
        if c == seqs - 1:
            for s in range(1, n):
                a_gather(c, s)
        ffn(c)
        ffn_back(c)
        if c >= 1:
            c_reduce(c - 1)
        if c >= 2:
            for s in range(1, n):
                c_gather(c - 2, s)
    for c in range(seqs):
        ffn_out(c)
        if c == 0:
            c_reduce(seqs - 1)
            if seqs >= 2:
                c_gather(seqs - 2, 1)
        elif seqs >= 2 and c + 1 < n:
            c_gather(seqs - 2, c + 1)
    if seqs >= 2:
        for s in range(seqs + 1, n):
            c_gather(seqs - 2, s)
    for s in range(1, n):
        c_gather(seqs - 1, s)
    for u in range(seqs * HALVES):
        line_a.rs_drain(u)
        line_a.ag_drain(u)
        line_c.rs_drain(u)
        line_c.ag_drain(u)
    for c in range(seqs):
        for d in range(1, slices):

            @pl.when(mine + d < slices)
            def _():
                kv_copy(c, d).wait_send()


def backward_kernel(
    seqs,
    tokens,
    qseg,
    kseg,
    na,
    wqkv,
    w_out,
    cos,
    sin,
    qpad,
    kv,
    lse,
    attpad,
    hidden_own,
    ffn_part,
    gh_own,
    ghb,
    block_out,
    input_grad,
    lin,
    attn_gain,
    part_b,
    rbuf_b,
    part_d,
    rbuf_d,
    own,
    dkv,
    dkv_send,
    dkv_recv,
    b_rs_s,
    b_rs_r,
    b_ag_s,
    b_ag_r,
    d_rs_s,
    d_rs_r,
    d_ag_s,
    d_ag_r,
    kv_s,
    kv_r,
):
    n = lax.axis_size("tensor")
    me = lax.axis_index("tensor")
    slices, mine = lax.axis_size("context"), lax.axis_index("context")
    rows = tokens.shape[0] // seqs
    width = tokens.shape[1]
    qw = w_out.shape[0]
    heads = qw // HEAD
    kvh = heads // 2
    pairw = wqkv.shape[1] - qw
    shard = rows // HALVES // n
    scale = 1.0 / math.sqrt(HEAD)
    line_b = Line("tensor", part_b, rbuf_b, block_out, b_rs_s, b_rs_r, b_ag_s, b_ag_r)
    line_d = Line("tensor", part_d, rbuf_d, input_grad, d_rs_s, d_rs_r, d_ag_s, d_ag_r)
    enter(True)
    step = 512

    def rows_of(c):
        return pl.ds(c * rows, rows)

    def units(c):
        return range(c * HALVES, (c + 1) * HALVES)

    def b_begin(c):
        for u in units(c):
            part_b[u] = ffn_part[u]
            line_b.rs_start(u)

    def b_reduce(c):
        for t in range(n - 1):
            for u in units(c):
                line_b.rs_step(u, t)
        for u in units(c):
            line_b.rs_own(u, own)
            block_out[u, me] = (own[...] + hidden_own[u]).astype(BF16)
            line_b.ag_start(u)

    def b_gather(c, s):
        for u in units(c):
            line_b.ag_step(u, s)

    def dkv_copy(c, d, target):
        return pltpu.make_async_remote_copy(
            src_ref=dkv_send.at[c, d - 1],
            dst_ref=dkv_recv.at[c, d - 1],
            send_sem=kv_s.at[c, d - 1],
            recv_sem=kv_r.at[c, d - 1],
            device_id={"context": target},
            device_id_type=MESH,
        )

    def attend_back(c):
        ga = mm_nt(ghb[pl.ds(c * HALVES, HALVES)].reshape(rows, width), w_out[...])
        qs = qseg[c]
        dqs = []
        bias0 = twice(mask_of(qs, kseg[c, mine], True))
        do_all = [take_head(ga, h).astype(BF16) for h in range(heads)]
        for g in range(kvh):
            do = jnp.concatenate([do_all[2 * g], do_all[2 * g + 1]], axis=0)
            att = attpad[c, 2 * g : 2 * g + 2].reshape(2 * rows, PAD)
            delta = jnp.sum(do.astype(F32) * att.astype(F32), axis=-1, keepdims=True)
            q2 = qpad[c, 2 * g : 2 * g + 2].reshape(2 * rows, PAD)
            top = lse[c, g]

            def grads(k, v, bias):
                s = mm_nt(q2, k) * scale + bias
                p = jnp.exp(s - top)
                ds = (p * (mm_nt(do, v) - delta) * scale).astype(BF16)
                return mm(ds, k), mm_tn(ds, q2), mm_tn(p.astype(BF16), do)

            dq, dk, dv = grads(kv[c, mine, g], kv[c, mine, kvh + g], bias0)
            dkv[g] = dk
            dkv[kvh + g] = dv

            def block(d, dq):
                b = mine - 1 - d
                bias = twice(mask_of(qs, kseg[c, b], False))
                more, dk, dv = grads(kv[c, b, g], kv[c, b, kvh + g], bias)
                dkv_send[c, d, g] = dk.astype(BF16)
                dkv_send[c, d, kvh + g] = dv.astype(BF16)
                return dq + more

            dq = lax.fori_loop(0, mine, block, dq)
            dqs += [dq[:rows], dq[rows:]]
        for d in range(1, slices):

            @pl.when(mine - d >= 0)
            def _():
                dkv_copy(c, d, mine - d).start()

        dq = put_heads(dqs, qw)
        ct, st = cos[rows_of(c), :], sin[rows_of(c), :]
        lin[rows_of(c), :qw] = (dq * ct - swap_halves(dq) * st).astype(BF16)
        for d in range(1, slices):

            @pl.when(mine + d < slices)
            def _():
                dkv_copy(c, d, mine + d).wait_recv()
                for h in range(2 * kvh):
                    dkv[h] = dkv[h] + dkv_recv[c, d - 1, h].astype(F32)

        p = put_heads([dkv[h] for h in range(2 * kvh)], pairw)
        back = p * ct[:, :pairw] - swap_halves(p) * st[:, :pairw]
        p = jnp.where(lane_of(p.shape) < kvh * HEAD, back, p)
        lin[rows_of(c), qw:] = p.astype(BF16)

    def d_begin(c):
        x = lin[rows_of(c), :]
        for t in range(0, width, step):
            part_d[pl.ds(c * HALVES, HALVES), :, :, t : t + step] = (
                mm_nt(x, wqkv[t : t + step, :]).astype(BF16).reshape(HALVES, n, shard, step)
            )
        for u in units(c):
            line_d.rs_start(u)

    def d_reduce(c):
        for t in range(n - 1):
            for u in units(c):
                line_d.rs_step(u, t)
        for u in units(c):
            line_d.rs_own(u, own)
            g = own[...]
            start = pl.multiple_of(u * n * shard + me * shard, shard)
            x = tokens[pl.ds(start, shard), :].astype(F32)
            inv = lax.rsqrt(jnp.mean(x * x, axis=-1, keepdims=True) + EPS)
            attn_gain[...] += jnp.sum(g * x * inv, axis=0, keepdims=True)
            scaled = g * na[...]
            input_grad[u, me] = (
                gh_own[u]
                + inv * scaled
                - x * (inv * inv * inv) * jnp.mean(scaled * x, axis=-1, keepdims=True)
            ).astype(BF16)
            line_d.ag_start(u)

    def d_gather(c, s):
        for u in units(c):
            line_d.ag_step(u, s)

    attn_gain[...] = jnp.zeros_like(attn_gain)
    for c in range(seqs):
        b_begin(c)
    for c in range(seqs):
        attend_back(c)
        d_begin(c)
        b_reduce(c)
        if c >= 1:
            d_reduce(c - 1)
            for s in range(1, n):
                b_gather(c - 1, s)
        if c >= 2:
            for s in range(1, n):
                d_gather(c - 2, s)
    d_reduce(seqs - 1)
    for s in range(1, n):
        b_gather(seqs - 1, s)
        if seqs >= 2:
            d_gather(seqs - 2, s)
    for s in range(1, n):
        d_gather(seqs - 1, s)
    for u in range(seqs * HALVES):
        line_b.rs_drain(u)
        line_b.ag_drain(u)
        line_d.rs_drain(u)
        line_d.ag_drain(u)
    for c in range(seqs):
        for d in range(1, slices):

            @pl.when(mine - d >= 0)
            def _():
                dkv_copy(c, d, mine - d).wait_send()


def rope_tables(positions, copies):
    steps = jnp.arange(HEAD // 2).astype(F32)
    inverse = THETA ** (-2.0 * steps / HEAD)
    angles = positions.astype(F32)[:, None] * inverse
    c, s = jnp.cos(angles), jnp.sin(angles)
    return (
        jnp.tile(jnp.concatenate([c, c], axis=1), (1, copies)),
        jnp.tile(jnp.concatenate([-s, s], axis=1), (1, copies)),
    )


def call(kernel, outs, scratch, ident, flops, args, out_specs=None):
    return pl.pallas_call(
        kernel,
        out_shape=outs,
        in_specs=[pl.BlockSpec(memory_space=VMEM)] * len(args),
        out_specs=[pl.BlockSpec(memory_space=VMEM)] * len(outs),
        scratch_shapes=scratch,
        compiler_params=pltpu.CompilerParams(
            collective_id=ident, has_side_effects=True, vmem_limit_bytes=67000000
        ),
        cost_estimate=pl.CostEstimate(
            flops=flops, bytes_accessed=50000000, transcendentals=0
        ),
    )(*args)


def on_device(
    tokens,
    cotangent,
    segments,
    positions,
    norm_attn,
    w_query,
    key_weight,
    value_weight,
    w_out,
    norm_ffn,
    w_gate,
    w_up,
    w_down,
):
    seqs, length, width = tokens.shape
    rows = seqs * length
    n, slices = lax.axis_size("tensor"), lax.axis_size("context")
    qw, pairw = w_query.shape[1], key_weight.shape[1] + value_weight.shape[1]
    heads, kvh = qw // HEAD, key_weight.shape[1] // HEAD
    hidden = w_gate.shape[1]
    units = seqs * HALVES
    shard = length // HALVES // n
    mine = lax.axis_index("context")

    tok = tokens.reshape(rows, width)
    cot = cotangent.reshape(rows, width)
    cos, sin = rope_tables(positions.reshape(rows), heads)
    wqkv = jnp.concatenate([w_query, key_weight, value_weight], axis=1)
    kseg = segments.reshape(seqs, slices, 1, length)
    qseg = lax.dynamic_slice_in_dim(segments, mine * length, length, 1)[..., None]
    na = norm_attn.astype(F32).reshape(1, width)
    nf = norm_ffn.astype(F32).reshape(1, width)

    def arr(shape, kind=BF16):
        return jax.ShapeDtypeStruct(shape, kind)

    line = (units, n, shard, width)
    half = (units, 2, n - 1, shard, width)
    fwd = call(
        functools.partial(forward_kernel, seqs),
        [
            arr((rows, width)),
            arr((seqs, heads, length, PAD)),
            arr((seqs, slices, 2 * kvh, length, PAD)),
            arr((seqs, kvh, 2 * length, 1), F32),
            arr((rows, qw)),
            arr((seqs, heads, length, PAD)),
            arr((units, shard, width), F32),
            arr(line),
            arr((rows, hidden)),
            arr((rows, hidden)),
            arr((rows, hidden)),
            arr(line),
            arr((units, shard, width), F32),
            arr(line),
            arr((1, width), F32),
        ],
        [
            pltpu.VMEM(line, BF16),
            pltpu.VMEM(half, BF16),
            pltpu.VMEM(line, BF16),
            pltpu.VMEM(half, BF16),
            pltpu.VMEM((rows, hidden), F32),
            pltpu.VMEM((shard, width), F32),
        ]
        + line_sems(units, n)
        + line_sems(units, n)
        + [
            pltpu.SemaphoreType.DMA((seqs, slices - 1)),
            pltpu.SemaphoreType.DMA((seqs, slices - 1)),
        ],
        0,
        2 * rows * width * (6 * hidden + 3 * qw),
        (tok, cot, qseg, kseg, na, nf, wqkv, w_out, w_gate, w_up, w_down, cos, sin),
    )
    (
        normed_attn,
        qpad,
        kv,
        lse,
        attended,
        attpad,
        hidden_own,
        normed_ffn,
        act,
        ggate,
        gup,
        ffn_part,
        gh_own,
        ghb,
        ffn_gain,
    ) = fwd
    bwd = call(
        functools.partial(backward_kernel, seqs),
        [arr(line), arr(line), arr((rows, qw + pairw)), arr((1, width), F32)],
        [
            pltpu.VMEM(line, BF16),
            pltpu.VMEM(half, BF16),
            pltpu.VMEM(line, BF16),
            pltpu.VMEM(half, BF16),
            pltpu.VMEM((shard, width), F32),
            pltpu.VMEM((2 * kvh, length, PAD), F32),
            pltpu.VMEM((seqs, slices - 1, 2 * kvh, length, PAD), BF16),
            pltpu.VMEM((seqs, slices - 1, 2 * kvh, length, PAD), BF16),
        ]
        + line_sems(units, n)
        + line_sems(units, n)
        + [
            pltpu.SemaphoreType.DMA((seqs, slices - 1)),
            pltpu.SemaphoreType.DMA((seqs, slices - 1)),
        ],
        1,
        2 * rows * width * 3 * qw,
        (
            tok,
            qseg,
            kseg,
            na,
            wqkv,
            w_out,
            cos,
            sin,
            qpad,
            kv,
            lse,
            attpad,
            hidden_own,
            ffn_part,
            gh_own,
            ghb,
        ),
    )
    block_out, input_grad, lin, attn_gain = bwd
    both = ("dp", "context")

    def summed(a, b):
        return lax.psum(mm_tn(a, b).astype(BF16), both)

    x = normed_ffn.reshape(rows, width)
    down_grad = summed(act, cot)
    gate_grad = summed(x, ggate)
    up_grad = summed(x, gup)
    out_grad = summed(attended, ghb.reshape(rows, width))
    query_grad = summed(normed_attn, lin[:, :qw])
    key_grad = summed(normed_attn, lin[:, qw : qw + pairw // 2])
    value_grad = summed(normed_attn, lin[:, qw + pairw // 2 :])
    gains = lax.psum(jnp.concatenate([attn_gain, ffn_gain]), ("dp", "context", "tensor"))
    return (
        block_out.reshape(seqs, length, width),
        input_grad.reshape(seqs, length, width),
        gains[0],
        query_grad.astype(F32),
        key_grad.astype(F32),
        value_grad.astype(F32),
        out_grad.astype(F32),
        gains[1],
        gate_grad.astype(F32),
        up_grad.astype(F32),
        down_grad.astype(F32),
    )


def solution(mesh):
    placed = (
        P("dp", "context", None),
        P("dp", "context", None),
        P("dp", None),
        P("dp", "context"),
        P(),
        P(None, "tensor"),
        P(None, "tensor"),
        P(None, "tensor"),
        P("tensor", None),
        P(),
        P(None, "tensor"),
        P(None, "tensor"),
        P("tensor", None),
    )
    return jax.shard_map(
        on_device,
        mesh=mesh,
        in_specs=placed,
        out_specs=(
            P("dp", "context", None),
            P("dp", "context", None),
            P(),
            P(None, "tensor"),
            P(None, "tensor"),
            P(None, "tensor"),
            P("tensor", None),
            P(),
            P(None, "tensor"),
            P(None, "tensor"),
            P("tensor", None),
        ),
        check_vma=False,
    )
```

time: 899 us -> 800 us (0.89)
  Pallas kernels: 0 us -> 546 us
  waiting for transfers between devices: 652 us -> 136 us
  matrix products: 78 us -> 21.6 us
  local copies, waits for them, and re-layouts: 66.8 us -> 12.8 us
  other arithmetic: 49.9 us -> 21.3 us
  blocking collectives: 25.9 us -> 38.1 us
    pallas_call x0 -> x2, Pallas kernels: none -> 546 us  [call(): pl.pallas_call(kernel, out_shape=outs, in_specs=[pl.BlockSpec(memory_spac...]
    psum x4 -> x1, waiting for transfers between devices: 614 us -> 136 us  [summed(): return lax.psum(mm_tn(a, b).astype(BF16), both)]
    dot_general x28 -> x7, matrix products: 78 us -> 21.6 us  [mm_tn(): lax.dot_general(a, b, (((0,), (0,)), ((), ())), preferred_element_type=F32)]
    unnamed x119 -> x52, local copies, waits for them, and re-layouts: 35.9 us -> 6.45 us
    all_gather x1 -> x0, waiting for transfers between devices: 23.4 us -> none  [on_device(): pair_all = lax.all_gather(pair_local, 'context', axis=1, tiled=True)]
    reduce_sum x6 -> x0, other arithmetic: 20.6 us -> none  [the longest x1 4.96 us: on_device(): ffn_gain_grad = jnp.sum(grad_normed_ffn * hidden_res * inv_ffn, axis=0)]
    ppermute x1 -> x0, waiting for transfers between devices: 14.2 us -> none  [shifted(): return lax.ppermute(x, axis, pairs)]
    psum x1, blocking collectives: 25.9 us -> 38.1 us  [on_device(): lax.psum(jnp.concatenate([attn_gain, ffn_gain]), ('dp', 'context', 'tenso...]
  transfers between devices with their start and end apart: 6 -> 1, of which waited for: 6 -> 1; matrix products, arithmetic and copies ran while one was open for 7% -> 0% of each run, Pallas kernels for 0% -> 0%
where the time goes in v1:
time: 800 us; the launch traced here: 791 us
  Pallas kernels  546 us (68%)
  waiting for transfers between devices  136 us (17%)
  blocking collectives  38.1 us (5%)
  matrix products  21.6 us (3%)
  other arithmetic  21.3 us (3%)
  between operations  14.6 us (2%)
  local copies, waits for them, and re-layouts  12.8 us (2%)
    pallas_call x2, Pallas kernels, call(): pl.pallas_call(kernel, out_shape=outs, in_specs=[pl.BlockSpec(memory_spac...  546 us
    psum x1, waiting for transfers between devices, summed(): return lax.psum(mm_tn(a, b).astype(BF16), both)  136 us
    psum x1, blocking collectives, on_device(): lax.psum(jnp.concatenate([attn_gain, ffn_gain]), ('dp', 'context', 'tenso...  38.1 us
    dot_general x7, matrix products, mm_tn(): lax.dot_general(a, b, (((0,), (0,)), ((), ())), preferred_element_type=F32)  21.6 us
  transfers between devices with their start and end apart: 1, of which 1 were waited for; matrix products, arithmetic and copies ran while one was open for 0% of the time, Pallas kernels for 0%

profile of v1, /device:TPU:0, one launch (start us, length us, event | category | flops | bytes accessed | tf_op | source)
XLA Modules:
  0.0 791.1 jit_solution(16322487091259842991)
XLA Ops:
  7.2 0.0 all-reduce.3.cloned.1.call-start
  7.2 0.7 convert_element_type.61
  7.9 0.6 fusion.3
  8.6 0.1 tile.8
  8.7 1.4 copy.32.cos
  10.1 0.1 tile.20
  10.2 0.0 copy-start.15
  10.2 0.0 copy-start.16
  10.2 0.0 copy-start.5
  10.2 1.4 copy.33.sin
  11.6 0.0 copy-done.12
  11.6 0.6 reshape.75.kseg
  12.2 0.9 copy.31.qseg
  13.1 0.0 copy-done.10
  13.1 0.3 copy.26
  13.4 1.3 copy.27
  14.8 0.0 copy-done.15
  14.8 0.6 reshape.86.na
  15.4 0.0 copy-done.16
  15.4 0.6 reshape.88.nf
  16.0 0.0 copy-done.5
  16.0 1.9 pad_maximum_fusion.wqkv
  17.9 278.5 %shard_map.212 = (bf16[768,1536]{1,0:T(8,128)(2,1)}, bf16[3,4,256,128]{3,2,1,0:T(8,128)(2,1)}, bf16[3,2,4,256,128]{4,3,2,1,0:T(8,128)(2,1)}, f32[3,2,512,1]{3,2,...) custom-call(bf16[768,1536]{1,0:T(8,128)(2,1)} %bitcast.26, ...), custom_call_target="tpu_custom_call" | custom-call | flops 17213423616 | bytes 50000000 | tf_op jit(solution)/shard_map/pallas_call | solution.py:790
  296.4 267.7 %shard_map.213 = (bf16[6,4,32,1536]{3,2,1,0:T(8,128)(2,1)}, bf16[6,4,32,1536]{3,2,1,0:T(8,128)(2,1)}, bf16[768,768]{1,0:T(8,128)(2,1)}, f32[1,1536]{1,0:T(1,128)}) custom-call(bf16[768,1536]{1,0:T(8,128)(2,1)} %bitcast.27, s32[3,256,1]{2,1,0:T(8,128)} %copy.31.qseg, s32[3,2,1,256]{3,2,1,0:T(1,128)} %reshape.75.kseg, f32[1,1536]{1,0:T(1,128)} %reshape.86.na, ...), custom_call_target="tpu_custom_call" | custom-call | flops 2717908992 | bytes 50000000 | tf_op jit(solution)/shard_map/pallas_call | solution.py:790
  564.1 0.0 copy-start.18
  564.1 0.0 copy-start.20
  564.1 3.4 convolution_convert_fusion.5
  567.5 0.0 copy-done.18
  567.5 0.0 copy-done.20
  567.5 1.5 convolution_convert_fusion.6
  569.0 2.4 convolution_convert_fusion.4
  571.5 0.0 copy-done.19
  571.5 0.0 copy-done.23
  571.5 4.0 convolution_convert_fusion.1
  575.5 0.0 copy-done.22
  575.5 4.0 convolution_convert_fusion.2
  579.6 0.0 copy-done.17
  579.6 0.0 copy-done.21
  579.6 4.1 convolution_convert_fusion
  583.7 0.0 copy-done
  583.7 0.0 copy-done.11
  583.7 2.1 convolution_convert_fusion.3
  585.8 0.0 all-reduce.3.cloned.1.call-update
  585.8 0.7 copy-done.13
  586.5 0.0 copy-done.14
  586.5 38.1 %psum.56 = f32[2,1536]{1,0:T(2,128)S(1)} all-reduce(f32[2,1536]{1,0:T(2,128)S(1)} %pad_maximum_fusion.3), channel_id=1, replica_groups=mesh['dp'=4,'context'=2,'tensor'=4] {'dp','context','tensor'}, use_global_device_ids=true, to_apply=%region_0.0 | all-reduce | flops 3072 | bytes 24576 | tf_op jit(solution)/shard_map/psum | solution.py:952
  624.6 0.6 slice_reduce_fusion
  625.2 136.4 %all-reduce.3.cloned.1.call-done = (bf16[1536,384]{1,0:T(8,128)(2,1)}, bf16[1536,192]{0,1:T(8,128)(2,1)}, bf16[1536,192]{0,1:T(8,128)(2,1)}, bf16[384,1536]{1,0:...) async-done(((bf16[1536,384]{1,0:T(8,128)(2,1)}, bf16[1536,192]{0,1:T(8,128)(2,1)}, bf16[1536,192]{0,1:T(8,128)(2,1)}, ...) | async-done | bytes 12976144 | tf_op jit(solution)/shard_map/psum | solution.py:942
  761.6 5.5 convert_element_type.73
  767.1 0.0 copy-done.2
  767.1 3.5 convert_element_type.75
  770.6 0.0 copy-done.1
  770.6 3.6 convert_element_type.77
  774.2 0.0 copy-done.7
  774.2 1.6 convert_element_type.65
  775.7 0.2 copy-done.6
  775.9 1.7 convert_element_type.71
  777.6 1.1 convert_element_type.67
  778.7 0.0 copy-done.8
  778.7 1.1 convert_element_type.69
  779.9 0.0 copy-done.4
  779.9 1.4 copy.43
  781.3 1.1 copy-done.3
  782.4 1.4 copy.44
  (25 shorter events, 0.1 us)
Async XLA Ops:
  7.2 754.5 %all-reduce.3.cloned.1.call-start = ((), (), s32[]{:S(2)}) async-start(), calls=%async_computation | async-start | bytes 25952256 | tf_op jit(solution)/shard_map/psum | solution.py:942
  10.1 1.5 copy-start.12
  10.1 3.1 copy-start.10
  10.2 4.6 copy-start.15
  10.2 5.2 copy-start.16
  10.2 5.8 copy-start.5
  564.1 3.4 copy-start.18
  564.1 3.4 copy-start.20
  569.0 2.5 copy-start.19
  569.0 2.5 copy-start.23
  571.5 4.0 copy-start.22
  575.5 4.0 copy-start.17
  575.5 4.0 copy-start.21
  579.6 4.1 copy-start
  579.6 4.1 copy-start.11
  585.8 0.7 copy-start.13
  585.8 0.7 copy-start.14
  761.6 5.5 copy-start.2
  767.1 3.5 copy-start.1
  770.6 3.6 copy-start.7
  774.2 1.7 copy-start.6
  775.7 1.9 copy-start.9
  775.9 2.8 copy-start.8
  777.6 2.3 copy-start.4
  779.9 2.5 copy-start.3
Sparse Core Ops, SparseCore 0:
  585.9 175.6 all-reduce.2
